TPU v7x, 32 devices: a whole 2x2x4 slice. The times are simulated.
32 devices in a mesh: dom: 16 (over z, y, core), sub: 2 (over x).
Axes of the slice: x: 2, y: 2, z: 4, core: 2. Of those that a mesh axis runs over, the one named last changes fastest.
Arguments:
- solution: float32 [125, 5, 1024], P(None, None, ('dom', 'sub')), may hold values from -1.2 to 5.4, as said below
- face_link: int32 [6, 1024], P(None, ('dom', 'sub')), may hold values from 0 to 6143, as said below
Outputs:
- rate: float32 [125, 5, 1024], P(None, None, ('dom', 'sub'))
Inputs may be any that keep to these rules, and one draw needn't show every extreme that they name: At every solution point density lies between 0.6 and 1.4, each velocity component between -0.8 and 0.8 and pressure between 0.6 and 1.6; at every flux point the interpolated density and pressure stay at 0.5 or more and each interpolated velocity component between -1.1 and 1.1. `face_link`: the pairing is mutual and pairs face 2 a + 1 of one element with face 2 a of another, point for point. Elements are numbered device by device in the order of the joined axes, 32 to a device; a partner lies in the same partition or in one whose dom index differs by at most 2 cyclically. At most 6 faces of one device pair with faces of any one other device, and in every draw some pair of devices reaches 6.
All inputs are finite; a program needn't handle non-finite values.
Results may differ from a plain program's by a relative error of at most 0.0003.
Values sent between devices are 32-bit elements; how exact they have to be, the bound alone decides.
A program may use at most 64 MiB of HBM per device.

v0:
```python
import jax
import jax.numpy as jnp
import numpy as np
from jax import lax
from jax.sharding import PartitionSpec as P

ORDER = 4


heat_ratio = 1.4
viscosity = 0.08
prandtl = 0.72
penalty = 0.1


def passed_along(block, axis, distance):
    devices = range(lax.axis_size(axis))
    route = [((i - distance) % len(devices), i) for i in devices]
    return lax.ppermute(block, axis, route)


def legendre_table(degree, abscissae):
    values = [abscissae * 0.0 + 1.0, abscissae.copy()]
    slopes = [abscissae * 0.0, abscissae * 0.0 + 1.0]
    for current in range(1, degree):
        values.append(
            ((2 * current + 1) * abscissae * values[current] - current * values[current - 1])
            / (current + 1)
        )
        slopes.append(slopes[current - 1] + (2 * current + 1) * values[current])
    return (values, slopes)


def gauss_nodes(degree):
    abscissae = np.cos(np.pi * (np.arange(degree) + 0.75) / (degree + 0.5))
    for unused in range(60):
        values, slopes = legendre_table(degree, abscissae)
        abscissae = abscissae - values[degree] / slopes[degree]
    return np.sort(abscissae)


def operator_tables(degree):
    abscissae = gauss_nodes(degree)
    differ = abscissae[:, None] - abscissae[None, :]
    padded = differ + np.eye(degree)
    weights = 1.0 / np.prod(padded, axis=1)
    derivative = weights[None, :] / weights[:, None] / padded * (1.0 - np.eye(degree))
    derivative = derivative - np.eye(degree) * np.sum(derivative, axis=1)[:, None]
    basis_left = weights / (-1.0 - abscissae)
    basis_left = basis_left / np.sum(basis_left)
    basis_right = weights / (1.0 - abscissae)
    basis_right = basis_right / np.sum(basis_right)
    values, slopes = legendre_table(degree, abscissae)
    right_slope = 0.5 * (slopes[degree - 1] + slopes[degree])
    mirror_values, mirror_slopes = legendre_table(degree, -abscissae)
    left_slope = -0.5 * (mirror_slopes[degree - 1] + mirror_slopes[degree])
    sol_points = degree**3
    face_points = degree**2
    interp = np.zeros((6 * face_points, sol_points))
    grad_matrix = np.zeros((3 * sol_points, sol_points))
    lift_matrix = np.zeros((3 * sol_points, 6 * face_points))
    div_lift = np.zeros((sol_points, 6 * face_points))
    for sol_index in range(sol_points):
        position = (sol_index // face_points, sol_index // degree % degree, sol_index % degree)
        for direction in range(3):
            others = [position[other_dir] for other_dir in range(3) if other_dir != direction]
            flux_index = others[0] * degree + others[1]
            along_index = position[direction]
            for facing in range(2):
                column = (2 * direction + facing) * face_points + flux_index
                interp[column, sol_index] = (basis_left, basis_right)[facing][along_index]
                correct = (left_slope, right_slope)[facing][along_index]
                lift_matrix[direction * sol_points + sol_index, column] = correct
                div_lift[sol_index, column] = (2 * facing - 1) * correct
            for target in range(degree):
                shifted = list(position)
                shifted[direction] = target
                other_point = (shifted[0] * degree + shifted[1]) * degree + shifted[2]
                grad_matrix[direction * sol_points + sol_index, other_point] = derivative[
                    along_index, target
                ]
    normal_matrix = np.zeros((6 * face_points, 3 * sol_points))
    normals = np.zeros((3, 6))
    for face_id in range(6):
        direction = face_id // 2
        orient = 2 * (face_id % 2) - 1
        rows_here = slice(face_id * face_points, (face_id + 1) * face_points)
        normal_matrix[rows_here, direction * sol_points : (direction + 1) * sol_points] = (
            orient * interp[rows_here]
        )
        normals[direction, face_id] = orient
    div_matrix = np.concatenate(
        [
            grad_matrix[direction * sol_points : (direction + 1) * sol_points]
            for direction in range(3)
        ],
        axis=1,
    )
    tables = (interp, grad_matrix, lift_matrix, normal_matrix, div_matrix, div_lift, normals)
    return tuple((jnp.asarray(source, dtype=jnp.float32) for source in tables))


def exact_dot(matrix, operand):
    return jnp.dot(
        matrix, operand, precision=lax.Precision.HIGHEST, preferred_element_type=jnp.float32
    )


def face_layout(matrix, face_points, fields, elements):
    return jnp.transpose(matrix.reshape(6, face_points, fields, elements), (1, 2, 0, 3))


def matrix_layout(faces):
    face_points, fields, sides, elements = faces.shape
    return jnp.transpose(faces, (2, 0, 1, 3)).reshape(sides * face_points, fields * elements)


def split_fields(values):
    return [values[:, field_id] for field_id in range(values.shape[1])]


def primitive(fields):
    density = fields[0]
    velocity = [fields[1 + direction] / density for direction in range(3)]
    kinetic = 0.5 * (fields[1] * velocity[0] + fields[2] * velocity[1] + fields[3] * velocity[2])
    pressure = (heat_ratio - 1.0) * (fields[4] - kinetic)
    return (density, velocity, pressure)


def inviscid_flux(fields, velocity, pressure, direction):
    result = [fields[1 + direction]]
    for component in range(3):
        member = fields[1 + component] * velocity[direction]
        if component == direction:
            member = member + pressure
        result.append(member)
    result.append((fields[4] + pressure) * velocity[direction])
    return result


def viscous_terms(fields, density, velocity, slopes):
    vel_slope = [
        [
            (slopes[across][1 + component] - velocity[component] * slopes[across][0]) / density
            for across in range(3)
        ]
        for component in range(3)
    ]
    energy_slope = []
    for across in range(3):
        internal = (slopes[across][4] - fields[4] / density * slopes[across][0]) / density
        internal = internal - (
            velocity[0] * vel_slope[0][across]
            + velocity[1] * vel_slope[1][across]
            + velocity[2] * vel_slope[2][across]
        )
        energy_slope.append(internal)
    divergence = vel_slope[0][0] + vel_slope[1][1] + vel_slope[2][2]
    return (vel_slope, energy_slope, divergence)


def viscous_flux(velocity, vel_slope, energy_slope, divergence, direction):
    stress = []
    for component in range(3):
        member = viscosity * (vel_slope[component][direction] + vel_slope[direction][component])
        if component == direction:
            member = member - 2.0 / 3.0 * viscosity * divergence
        stress.append(member)
    work_done = velocity[0] * stress[0] + velocity[1] * stress[1] + velocity[2] * stress[2]
    heat_flux = viscosity * heat_ratio / prandtl * energy_slope[direction]
    return [jnp.zeros_like(divergence)] + stress + [work_done + heat_flux]


def total_flux(fields, slopes):
    density, velocity, pressure = primitive(fields)
    vel_slope, energy_slope, divergence = viscous_terms(fields, density, velocity, slopes)
    result = []
    for direction in range(3):
        inviscid = inviscid_flux(fields, velocity, pressure, direction)
        viscous = viscous_flux(velocity, vel_slope, energy_slope, divergence, direction)
        result.append([inviscid[field_id] - viscous[field_id] for field_id in range(5)])
    return result


def normal_viscous(fields, slopes, weights):
    density, velocity, pressure = primitive(fields)
    vel_slope, energy_slope, divergence = viscous_terms(fields, density, velocity, slopes)
    summed = [0.0] * 5
    for direction in range(3):
        viscous = viscous_flux(velocity, vel_slope, energy_slope, divergence, direction)
        summed = [
            summed[field_id] + weights[direction] * viscous[field_id] for field_id in range(5)
        ]
    return summed


def common_flux(own_fields, other_fields, own_visc, other_visc, weights):
    rho_left, vel_left, press_left = primitive(own_fields)
    rho_right, vel_right, press_right = primitive(other_fields)
    normal_left = [0.0] * 5
    normal_right = [0.0] * 5
    speed_left = 0.0
    speed_right = 0.0
    for direction in range(3):
        flux_left = inviscid_flux(own_fields, vel_left, press_left, direction)
        flux_right = inviscid_flux(other_fields, vel_right, press_right, direction)
        normal_left = [
            normal_left[field_id] + weights[direction] * flux_left[field_id]
            for field_id in range(5)
        ]
        normal_right = [
            normal_right[field_id] + weights[direction] * flux_right[field_id]
            for field_id in range(5)
        ]
        speed_left = speed_left + weights[direction] * vel_left[direction]
        speed_right = speed_right + weights[direction] * vel_right[direction]
    wave_left = jnp.abs(speed_left) + jnp.sqrt(heat_ratio * press_left / rho_left)
    wave_right = jnp.abs(speed_right) + jnp.sqrt(heat_ratio * press_right / rho_right)
    wave_speed = jnp.maximum(wave_left, wave_right)
    return [
        0.5 * (normal_left[field_id] + normal_right[field_id])
        - 0.5 * (own_visc[field_id] + other_visc[field_id])
        + (0.5 * wave_speed + penalty) * (own_fields[field_id] - other_fields[field_id])
        for field_id in range(5)
    ]


def group_rank(group_of, sort_key, groups, span):
    length = group_of.shape[0]
    ordering = jnp.argsort(group_of * span + sort_key)
    sorted_group = group_of[ordering]
    group_ids = jnp.arange(groups, dtype=jnp.int32)
    member_hits = (group_of[:, None] == group_ids[None, :]).astype(jnp.int32)
    counts = jnp.sum(member_hits, axis=0)
    starts = jnp.cumsum(counts) - counts
    group_start = jnp.sum(
        jnp.where(sorted_group[:, None] == group_ids[None, :], starts[None, :], 0), axis=1
    )
    ranked = jnp.arange(length, dtype=jnp.int32) - group_start
    return jnp.zeros((length,), jnp.int32).at[ordering].set(ranked)


def plan_routes(face_link, sub_count, dom_count, capacity):
    elements = face_link.shape[1]
    face_total = 6 * elements
    link_flat = face_link.reshape(face_total)
    partner_elem = link_flat // 6
    partner_dev = partner_elem // elements
    partner_key = link_flat % 6 * elements + partner_elem % elements
    my_dom = lax.axis_index("dom")
    my_sub = lax.axis_index("sub")
    is_local = partner_dev == my_dom * sub_count + my_sub
    partner_dom = partner_dev // sub_count
    partner_sub = partner_dev % sub_count
    ahead = (partner_dom - my_dom + 2) % dom_count - 2
    groups = 5 * sub_count + 1
    group_of = jnp.where(is_local, groups - 1, (ahead + 2) * sub_count + partner_sub)
    own_key = jnp.arange(face_total, dtype=jnp.int32)
    send_rank = group_rank(group_of, own_key, groups, face_total)
    recv_rank = group_rank(group_of, partner_key, groups, face_total)
    slot_total = 5 * sub_count * capacity
    send_slot = jnp.where(is_local, slot_total, group_of * capacity + send_rank)
    send_cols = (
        jnp.full((slot_total + 1,), face_total, jnp.int32).at[send_slot].set(own_key)[:slot_total]
    )
    recv_col = face_total + ((2 - ahead) * sub_count + partner_sub) * capacity + recv_rank
    gather_cols = jnp.where(is_local, partner_key, recv_col)
    return (send_cols.reshape(5, sub_count * capacity), gather_cols)


def deliver(face_vals, send_cols, gather_cols, swap_fn, move_fn):
    packed = jnp.take(face_vals, send_cols, axis=1, mode="fill", fill_value=0.0)
    arrived = swap_fn(jnp.moveaxis(packed, 1, 0))
    pieces = [face_vals]
    for slot_id in range(5):
        if slot_id == 2:
            pieces.append(arrived[2])
        else:
            pieces.append(move_fn(arrived[slot_id], slot_id - 2))
    source = jnp.concatenate(pieces, axis=1)
    return jnp.take(source, gather_cols, axis=1)


def shards(solution, face_link):
    interp, grad_matrix, lift_matrix, normal_matrix, div_matrix, div_lift, normals = (
        operator_tables(ORDER + 1)
    )
    sol_points, fields, elements = solution.shape
    face_points = (ORDER + 1) ** 2
    sub_count = lax.axis_size("sub")
    dom_count = lax.axis_size("dom")
    capacity = max(3, elements * 3 // 16)
    send_cols, gather_cols = plan_routes(face_link, sub_count, dom_count, capacity)
    weights = [normals[direction].reshape(1, 6, 1) for direction in range(3)]
    flat_sol = solution.reshape(sol_points, fields * elements)
    own_trace = face_layout(exact_dot(interp, flat_sol), face_points, fields, elements)
    other_trace = deliver(
        own_trace.reshape(face_points * fields, 6 * elements),
        send_cols,
        gather_cols,
        lambda shipment: lax.all_to_all(shipment, "sub", split_axis=2, concat_axis=2, tiled=True),
        lambda shipment, offset: passed_along(shipment, "dom", offset),
    ).reshape(face_points, fields, 6, elements)
    jump_mat = matrix_layout(0.5 * (other_trace - own_trace))
    grad_field = (exact_dot(grad_matrix, flat_sol) + exact_dot(lift_matrix, jump_mat)).reshape(
        3, sol_points, fields, elements
    )
    spread = jnp.einsum(
        "pq,dqx->dpx",
        interp,
        grad_field.reshape(3, sol_points, fields * elements),
        precision=lax.Precision.HIGHEST,
    )
    traced = jnp.transpose(spread.reshape(3, 6, face_points, fields, elements), (0, 2, 3, 1, 4))
    own_slopes = [split_fields(traced[direction]) for direction in range(3)]
    own_fields = split_fields(own_trace)
    other_fields = split_fields(other_trace)
    own_visc = normal_viscous(own_fields, own_slopes, weights)
    outgoing = jnp.stack(own_visc, axis=1).reshape(face_points * fields, 6 * elements)
    arrived = deliver(
        outgoing,
        send_cols,
        gather_cols,
        lambda shipment: lax.all_to_all(shipment, "sub", split_axis=2, concat_axis=2, tiled=True),
        lambda shipment, offset: passed_along(shipment, "dom", offset),
    ).reshape(face_points, fields, 6, elements)
    other_visc = [-member for member in split_fields(arrived)]
    sol_fields = split_fields(solution)
    sol_slopes = [split_fields(grad_field[direction]) for direction in range(3)]
    fluxes = total_flux(sol_fields, sol_slopes)
    flux_mat = jnp.stack([jnp.stack(fluxes[direction], axis=1) for direction in range(3)]).reshape(
        3 * sol_points, fields * elements
    )
    own_normal = face_layout(exact_dot(normal_matrix, flux_mat), face_points, fields, elements)
    common = common_flux(own_fields, other_fields, own_visc, other_visc, weights)
    flux_jump = matrix_layout(jnp.stack(common, axis=1) - own_normal)
    return -(exact_dot(div_matrix, flux_mat) + exact_dot(div_lift, flux_jump)).reshape(
        sol_points, fields, elements
    )


def solution(mesh):
    in_specs = (P(None, None, ("dom", "sub")), P(None, ("dom", "sub")))
    out_specs = P(None, None, ("dom", "sub"))
    return jax.shard_map(shards, mesh=mesh, in_specs=in_specs, out_specs=out_specs, check_vma=False)
```

profile of v0, /device:TPU:0, one launch (start us, length us, event | category | flops | bytes accessed | tf_op | source)
XLA Modules:
  0.0 68.6 jit_solution(7901080165753996893)
XLA Ops:
  0.0 0.7 %broadcast_remainder_fusion = (s32[6,32]{1,0:T(8,128)S(1)}, s32[6,32]{1,0:T(8,128)S(1)}) fusion(s32[6,32]{1,0:T(8,128)} %param.14), kind=kLoop, calls=%fused_computation.222 | loop fusion | flops 384 | bytes 2304 | tf_op jit(solution)/shard_map/jit(floor_divide)/rem | solution.py:247
  0.7 0.7 %sign_compare_fusion = pred[6,32]{1,0:T(8,128)(4,1)S(1)} fusion(s32[6,32]{1,0:T(8,128)} %param.14), kind=kLoop, calls=%fused_computation.213 | loop fusion | flops 384 | bytes 960 | tf_op jit(solution)/shard_map/jit(floor_divide)/ne | solution.py:247
  1.8 3.2 %sort.31 = (s32[192]{0:T(256)}, s32[192]{0:T(256)S(1)}) sort(s32[192]{0:T(256)S(1)} %iota_add_fusion, s32[192]{0:T(256)S(1)} %iota.24), dimensions={0}, to_apply=%region_0.1 | sort | flops 1536 | bytes 3072 | tf_op jit(solution)/shard_map/jit(argsort)/sort | solution.py:230
  5.0 3.2 %sort.32 = (s32[192]{0:T(256)}, s32[192]{0:T(256)S(1)}) sort(s32[192]{0:T(256)S(1)} %get-tuple-element.62, s32[192]{0:T(256)S(1)} %iota.27), dimensions={0}, to_apply=%region_6.8 | sort | flops 1536 | bytes 3072 | tf_op jit(solution)/shard_map/jit(argsort)/sort | solution.py:230
  8.2 1.6 %gather_fusion = s32[192]{0:T(256)S(1)} fusion(s32[192]{0:T(256)S(1)} %get-tuple-element.64, s32[1024]{0:T(1024)S(1)} %get-tuple-element.100), kind=kCustom, calls=%fused_computation.4 | custom fusion | bytes 2304 | tf_op jit(solution)/shard_map/gather | solution.py:231
  9.8 1.6 %gather_fusion.1 = s32[192]{0:T(256)S(1)} fusion(s32[192]{0:T(256)S(1)} %get-tuple-element.64, s32[1024]{0:T(1024)S(1)} %get-tuple-element.101), kind=kCustom, calls=%fused_computation.5 | custom fusion | bytes 2304 | tf_op jit(solution)/shard_map/gather | solution.py:231
  11.4 0.2 reduce-window.8
  11.7 1.2 %scatter_custom_fusion = s32[192]{0:T(256)S(1)} fusion(s32[192]{0:T(256)S(1)} %compare_select_fusion.4, s32[192]{0:T(256)S(1)} %iota_subtract_fusion.1, s32[]{:T(128)} %constant.141.clone.1), kind=kCustom, calls=%fused_computation.247 | custom fusion | bytes 772 | tf_op jit(solution)/shard_map/scatter | solution.py:240
  13.0 1.2 %scatter_custom_fusion.1 = s32[61]{0:T(128)S(1)} fusion(s32[192]{0:T(256)S(1)} %compare_select_fusion.3, s32[192]{0:T(256)S(1)} %iota.26, s32[]{:T(128)} %constant.138.clone.1), kind=kCustom, calls=%fused_computation.256 | custom fusion | bytes 248 | tf_op jit(solution)/shard_map/scatter | solution.py:264
  14.4 0.6 convolution_bitcast_fusion
  15.0 0.2 copy.75
  15.5 0.6 gather_fusion.2
  16.2 0.7 %fusion.56 = f32[5,125,12]{1,0,2:T(8,128)} fusion(f32[5,12,125]{2,1,0:T(8,128)S(1)} %reshape.273, pred[5,12]{0,1:T(8,128)(4,1)S(1)} %copy.76), kind=kLoop, calls=%fused_computation.139 | loop fusion | flops 7500 | bytes 60060 | tf_op jit(solution)/shard_map/transpose | solution.py:273
  16.9 4.2 %all-to-all-start = ((f32[5,125,12]{1,0,2:T(8,128)}), f32[5,125,12]{1,0,2:T(8,128)S(1)}, u32[]{:S(2)}, u32[]{:S(2)}) async-start(f32[5,125,12]{1,0,2:T(8,128)} %fusion.56), calls=%async_computation | async-start | bytes 98304 | tf_op jit(solution)/shard_map/all_to_all | solution.py:301
  21.1 0.6 constant_dynamic-update-slice_fusion.4
  21.7 1.2 %scatter_custom_fusion.2 = s32[192]{0:T(256)S(1)} fusion(s32[192]{0:T(256)S(1)} %compare_select_fusion.2, s32[192]{0:T(256)S(1)} %iota_subtract_fusion, s32[]{:T(128)} %constant.141.clone.1), kind=kCustom, calls=%fused_computation.249 | custom fusion | bytes 772 | tf_op jit(solution)/shard_map/scatter | solution.py:240
  23.0 0.7 %constant_dynamic-update-slice_fusion.19 = f32[25,5,6,32]{3,0,1,2:T(8,128)} fusion(f32[6]{0:T(128)S(1)} %copy-done.29), kind=kLoop, calls=%fused_computation.135 | loop fusion | bytes 98328
  23.7 0.4 fusion.114
  24.1 1.1 %all-to-all-done = f32[5,125,12]{1,0,2:T(8,128)S(1)} async-done(((f32[5,125,12]{1,0,2:T(8,128)}), f32[5,125,12]{1,0,2:T(8,128)S(1)}, u32[]{:S(2)}, u32[]{:S(2)}) %all-to-all-start) | async-done | bytes 30032 | tf_op jit(solution)/shard_map/all_to_all | solution.py:301
  25.2 5.1 %collective-permute-start = (f32[125,12]{0,1:T(8,128)S(1)}, f32[125,12]{0,1:T(8,128)S(1)}, u32[]{:S(2)}, u32[]{:S(2)}) collective-permute-start(f32[125,12]{0,1:T(8,128)S(1)} %bitcast.125), channel_id=1, source_target_pairs={{4,0},{6,2},{8,4},{10,6},{12,8},{14,10},{16,12},{18,14},{20,16},{2... | collective-permute-start | bytes 18008 | tf_op jit(solution)/shard_map/ppermute | solution.py:19
  30.3 0.5 collective-permute-start.2
  30.9 0.8 %collective-permute-done = f32[125,12]{0,1:T(8,128)S(1)} collective-permute-done((f32[125,12]{0,1:T(8,128)S(1)}, f32[125,12]{0,1:T(8,128)S(1)}, u32[]{:S(2)}, u32[]{:S(2)}) %collective-permute-start) | collective-permute-done | bytes 6032 | tf_op jit(solution)/shard_map/ppermute | solution.py:19
  31.8 4.3 %collective-permute-done.2 = f32[125,12]{0,1:T(8,128)S(1)} collective-permute-done((f32[125,12]{0,1:T(8,128)S(1)}, f32[125,12]{0,1:T(8,128)S(1)}, u32[]{:S(2)}, u32[]{:S(2)}) %collective-permute-start.2) | collective-permute-done | bytes 6032 | tf_op jit(solution)/shard_map/ppermute | solution.py:19
  36.1 1.1 %collective-permute-done.3 = f32[125,12]{0,1:T(8,128)S(1)} collective-permute-done((f32[125,12]{0,1:T(8,128)S(1)}, f32[125,12]{0,1:T(8,128)S(1)}, u32[]{:S(2)}, u32[]{:S(2)}) %collective-permute-start.3) | collective-permute-done | bytes 6032 | tf_op jit(solution)/shard_map/ppermute | solution.py:19
  37.2 0.2 concatenate.6
  37.4 0.7 %gather_fusion.3 = f32[192,125]{1,0:T(8,128)S(1)} fusion(f32[125,252]{0,1:T(8,128)S(1)} %concatenate.6, s32[1024]{0:T(1024)S(1)} %pad_clamp_fusion), kind=kCustom, calls=%fused_computation.1.clone | custom fusion | bytes 192768 | tf_op jit(solution)/shard_map/jit(_take)/gather | solution.py:281
  38.7 0.2 copy.87
  39.1 0.5 copy-done.8
  39.5 0.6 convolution_add_fusion
  40.1 0.2 reshape_reshape.3
  40.3 0.7 %fusion.111 = (f32[125,160]{0,1:T(8,128)}, f32[125,160]{0,1:T(8,128)S(1)}, f32[125,160]{0,1:T(8,128)}) fusion(f32[375,160]{0,1:T(8,128)S(1)} %convolution_add_fusion), kind=kLoop, calls=%fused_computation.259 | loop fusion | bytes 480000 | tf_op jit(solution)/shard_map/slice | solution.py:329
  41.1 0.6 convolution_bitcast_fusion.1
  41.6 0.3 reshape.182
  41.9 0.2 copy.206
  42.4 0.8 %copy-done.1 = f32[25,5,6,32]{3,0,1,2:T(8,128)S(1)} copy-done((f32[25,5,6,32]{3,0,1,2:T(8,128)S(1)}, f32[25,5,6,32]{3,0,1,2:T(8,128)}, u32[]{:S(2)}) %copy-start.1) | copy-done | bytes 96024
  43.2 0.8 %constant_dynamic-update-slice_fusion.18 = (f32[25,5,6,32]{3,0,1,2:T(8,128)S(1)}, f32[25,1,6,32]{3,0,1,2:T(8,128)}, f32[25,1,6,32]{3,0,1,2:T(8,128)S(1)}, f32[25...) fusion(f32[25,5,6,32]{3,0,1,2:T(8,128)S(1)} %copy-done.1, ...), kind=kLoop, calls=%fused_computation.134 | loop fusion | flops 177600 | bytes 2478336
  44.0 0.7 %constant_dynamic-update-slice_fusion.17 = (f32[25,5,6,32]{3,0,1,2:T(8,128)S(1)}, f32[25,1,6,32]{3,0,1,2:T(8,128)}, f32[25,1,6,32]{3,0,1,2:T(8,128)S(1)}, f32[25,1,6,32]{3,0,1,2:T(8,128)S(1)}) fusion(f32[25,5,6,32]{3,0,1,2:T(8,128)S(1)} %get-tuple-element.28, f32[6]{0:T(128)S(1)} %copy-done.31, f32[25,1,6,32]{3,0,1,2:T(8,128)S(1)} %get-tuple-element.36, ...), kind=kLoop, calls=%fused_computation.133 | loop fusion | flops 91200 | bytes 1495296
  44.8 0.7 %constant_dynamic-update-slice_fusion.16 = (f32[25,5,6,32]{3,0,1,2:T(8,128)S(1)}, f32[25,1,6,32]{3,0,1,2:T(8,128)}) fusion(f32[25,5,6,32]{3,0,1,2:T(8,128)S(1)} %get-tuple-element.24, f32[25,1,6,32]{3,0,1,2:T(8,128)S(1)} %get-tuple-element.36, f32[25,1,6,32]{3,0,1,2:T(8,128)S(1)} %get-tuple-element.38, f32[25,1,6,32]{3,0,1,2:T(8,128)S(1)} %get-tuple-element.34, ...), kind=kLoop, calls=%fused_computation.132 | loop fusion | flops 62400 | bytes 807168
  45.5 0.9 %constant_dynamic-update-slice_fusion.15 = (f32[25,5,6,32]{3,0,1,2:T(8,128)S(1)}, f32[25,1,6,32]{3,0,1,2:T(8,128)}) fusion(f32[25,5,6,32]{3,0,1,2:T(8,128)S(1)} %get-tuple-element.22, f32[25,1,6,32]{3,0,1,2:T(8,128)S(1)} %get-tuple-element.37, f32[25,1,6,32]{3,0,1,2:T(8,128)S(1)} %get-tuple-element.36, f32[25,1,6,32]{3,0,1,2:T(8,128)S(1)} %get-tuple-element.35, ...), kind=kLoop, calls=%fused_computation.131 | loop fusion | flops 345600 | bytes 2085120 | tf_op jit(solution)/shard_map/stack | solution.py:319
  46.4 0.2 copy.94
  46.9 0.2 copy-done.17
  47.1 0.6 gather_fusion.4
  47.7 0.7 %fusion.55 = f32[5,125,12]{1,0,2:T(8,128)} fusion(f32[5,12,125]{2,1,0:T(8,128)S(1)} %reshape.279, pred[5,12]{0,1:T(8,128)(4,1)S(1)} %copy-done.24), kind=kLoop, calls=%fused_computation.137 | loop fusion | flops 7500 | bytes 60060 | tf_op jit(solution)/shard_map/transpose | solution.py:273
  48.4 3.3 %all-to-all-start.1 = ((f32[5,125,12]{1,0,2:T(8,128)}), f32[5,125,12]{1,0,2:T(8,128)S(1)}, u32[]{:S(2)}, u32[]{:S(2)}) async-start(f32[5,125,12]{1,0,2:T(8,128)} %fusion.55), calls=%async_computation.1 | async-start | bytes 98304 | tf_op jit(solution)/shard_map/all_to_all | solution.py:324
  52.1 0.2 copy.88
  52.2 0.2 reshape.181
  52.4 0.4 copy-done.9
  52.8 0.4 fusion.116
  53.2 2.5 %all-to-all-done.1 = f32[5,125,12]{1,0,2:T(8,128)S(1)} async-done(((f32[5,125,12]{1,0,2:T(8,128)}), f32[5,125,12]{1,0,2:T(8,128)S(1)}, u32[]{:S(2)}, u32[]{:S(2)}) %all-to-all-start.1) | async-done | bytes 30032 | tf_op jit(solution)/shard_map/all_to_all | solution.py:324
  55.9 0.5 collective-permute-start.6
  56.4 2.0 %collective-permute-start.7 = (f32[125,12]{0,1:T(8,128)S(1)}, f32[125,12]{0,1:T(8,128)S(1)}, u32[]{:S(2)}, u32[]{:S(2)}) collective-permute-start(f32[125,12]{0,1:T(8,128)S(1)} %bitcast.128), channel_id=1, source_target_pairs={{28,0},{30,2},{0,4},{2,6},{4,8},{6,10},{8,12},{10,14},{12,16},{14,... | collective-permute-start | bytes 18008 | tf_op jit(solution)/shard_map/ppermute | solution.py:19
  58.4 0.4 fusion.115
  58.9 0.5 collective-permute-done.4
  59.5 2.3 %collective-permute-done.6 = f32[125,12]{0,1:T(8,128)S(1)} collective-permute-done((f32[125,12]{0,1:T(8,128)S(1)}, f32[125,12]{0,1:T(8,128)S(1)}, u32[]{:S(2)}, u32[]{:S(2)}) %collective-permute-start.6) | collective-permute-done | bytes 6032 | tf_op jit(solution)/shard_map/ppermute | solution.py:19
  61.8 1.0 %collective-permute-done.7 = f32[125,12]{0,1:T(8,128)S(1)} collective-permute-done((f32[125,12]{0,1:T(8,128)S(1)}, f32[125,12]{0,1:T(8,128)S(1)}, u32[]{:S(2)}, u32[]{:S(2)}) %collective-permute-start.7) | collective-permute-done | bytes 6032 | tf_op jit(solution)/shard_map/ppermute | solution.py:19
  62.8 0.2 concatenate.7
  63.0 1.0 %gather_fusion.5 = f32[192,125]{1,0:T(8,128)S(1)} fusion(f32[125,252]{0,1:T(8,128)S(1)} %concatenate.7, s32[1024]{0:T(1024)} %copy-done.25), kind=kCustom, calls=%fused_computation.3.clone | custom fusion | bytes 192768 | tf_op jit(solution)/shard_map/jit(_take)/gather | solution.py:281
  64.5 0.3 fusion.53
  64.8 0.5 copy-done.7
  65.8 0.5 copy-done.4
  66.3 0.2 fusion.33
  66.6 0.2 copy.113
  67.0 0.4 copy-done.12
  67.4 1.2 %fusion = f32[160,125]{1,0:T(8,128)} fusion(f32[160,125]{1,0:T(8,128)S(1)} %fusion.115, f32[150,160]{1,0:T(8,128)S(1)} %reshape.186, f32[125,150]{1,0:T(8,128)S(1)} %copy-done.12), kind=kOutput, calls=%fused_computation.14 | convolution fusion | flops 36040000 | bytes 331000 | tf_op jit(solution)/shard_map/dot_general | solution.py:104
  (134 shorter events, 4.1 us)
Async XLA Ops:
  0.0 14.3 %copy-start.14 = (f32[6,25,125,1]{2,1,3,0:T(8,128)S(1)}, f32[6,25,125,1]{2,1,3,0:T(8,128)}, u32[]{:S(2)}) copy-start(f32[6,25,125,1]{2,1,3,0:T(8,128)} %constant.181) | copy-start | bytes 225004
  0.0 14.3 %copy-start = (f32[125,5,32]{0,2,1:T(8,128)S(1)}, f32[125,5,32]{0,2,1:T(8,128)}, u32[]{:S(2)}) copy-start(f32[125,5,32]{0,2,1:T(8,128)} %param.13) | copy-start | bytes 240004
  14.4 1.7 %copy-start.16 = (s32[1024]{0:T(1024)}, s32[1024]{0:T(1024)S(1)}, u32[]{:S(2)}) copy-start(s32[1024]{0:T(1024)S(1)} %pad_clamp_fusion.1) | copy-start | bytes 12292
  15.5 7.5 %copy-start.29 = (f32[6]{0:T(128)S(1)}, f32[6]{0:T(128)}, u32[]{:S(2)}) copy-start(f32[6]{0:T(128)} %constant.177) | copy-start | bytes 76
  15.5 8.2 %copy-start.11 = (f32[375,125]{1,0:T(8,128)S(1)}, f32[375,125]{1,0:T(8,128)}, u32[]{:S(2)}) copy-start(f32[375,125]{1,0:T(8,128)} %constant.162.clone) | copy-start | bytes 562504
  16.2 0.7 %copy-start.23 = (pred[5,12]{0,1:T(8,128)(4,1)}, pred[5,12]{0,1:T(8,128)(4,1)S(1)}, u32[]{:S(2)}) copy-start(pred[5,12]{0,1:T(8,128)(4,1)S(1)} %copy.76) | copy-start | bytes 184
  16.9 8.3 %all-to-all-start = ((f32[5,125,12]{1,0,2:T(8,128)}), f32[5,125,12]{1,0,2:T(8,128)S(1)}, u32[]{:S(2)}, u32[]{:S(2)}) async-start(f32[5,125,12]{1,0,2:T(8,128)} %fusion.56), calls=%async_computation | async-start | bytes 98304 | tf_op jit(solution)/shard_map/all_to_all | solution.py:301
  24.1 14.3 %copy-start.26 = (pred[192]{0:T(512)(128)(4,1)}, pred[192]{0:T(512)(128)(4,1)S(1)}, u32[]{:S(2)}) copy-start(pred[192]{0:T(512)(128)(4,1)S(1)} %get-tuple-element.60) | copy-start | bytes 580
  25.2 6.5 %collective-permute-start = (f32[125,12]{0,1:T(8,128)S(1)}, f32[125,12]{0,1:T(8,128)S(1)}, u32[]{:S(2)}, u32[]{:S(2)}) collective-permute-start(f32[125,12]{0,1:T(8,128)S(1)} %bitcast.125), channel_id=1, source_target_pairs={{4,0},{6,2},{8,4},{10,6},{12,8},{14,10},{16,12},{18,14},{20,16},{2... | collective-permute-start | bytes 18008 | tf_op jit(solution)/shard_map/ppermute | solution.py:19
  30.3 1.4 %collective-permute-start.1 = (f32[125,12]{0,1:T(8,128)S(1)}, f32[125,12]{0,1:T(8,128)S(1)}, u32[]{:S(2)}, u32[]{:S(2)}) collective-permute-start(f32[125,12]{0,1:T(8,128)S(1)} %bitcast.127), channel_id=1, source_target_pairs={{2,0},{4,2},{6,4},{8,6},{10,8},{12,10},{14,12},{16,14},{18,16},{20... | collective-permute-start | bytes 18008 | tf_op jit(solution)/shard_map/ppermute | solution.py:19
  30.3 5.8 %collective-permute-start.2 = (f32[125,12]{0,1:T(8,128)S(1)}, f32[125,12]{0,1:T(8,128)S(1)}, u32[]{:S(2)}, u32[]{:S(2)}) collective-permute-start(f32[125,12]{0,1:T(8,128)S(1)} %bitcast.129), channel_id=1, source_target_pairs={{30,0},{0,2},{2,4},{4,6},{6,8},{8,10},{10,12},{12,14},{14,16},{16,... | collective-permute-start | bytes 18008 | tf_op jit(solution)/shard_map/ppermute | solution.py:19
  30.9 6.3 %collective-permute-start.3 = (f32[125,12]{0,1:T(8,128)S(1)}, f32[125,12]{0,1:T(8,128)S(1)}, u32[]{:S(2)}, u32[]{:S(2)}) collective-permute-start(f32[125,12]{0,1:T(8,128)S(1)} %bitcast.130), channel_id=1, source_target_pairs={{28,0},{30,2},{0,4},{2,6},{4,8},{6,10},{8,12},{10,14},{12,16},{14,... | collective-permute-start | bytes 18008 | tf_op jit(solution)/shard_map/ppermute | solution.py:19
  30.9 7.4 %copy-start.25 = (s32[1024]{0:T(1024)}, s32[1024]{0:T(1024)S(1)}, u32[]{:S(2)}) copy-start(s32[1024]{0:T(1024)S(1)} %pad_clamp_fusion) | copy-start | bytes 12292
  38.5 1.0 %copy-start.8 = (f32[375,150]{1,0:T(8,128)S(1)}, f32[375,150]{1,0:T(8,128)}, u32[]{:S(2)}) copy-start(f32[375,150]{1,0:T(8,128)} %constant.163.clone) | copy-start | bytes 675004
  38.9 2.2 %copy-start.15 = (f32[150,125,1]{1,0,2:T(8,128)S(1)}, f32[150,125,1]{1,0,2:T(8,128)}, u32[]{:S(2)}) copy-start(f32[150,125,1]{1,0,2:T(8,128)} %constant.182) | copy-start | bytes 225004
  42.2 1.0 %copy-start.1 = (f32[25,5,6,32]{3,0,1,2:T(8,128)S(1)}, f32[25,5,6,32]{3,0,1,2:T(8,128)}, u32[]{:S(2)}) copy-start(f32[25,5,6,32]{3,0,1,2:T(8,128)} %constant_dynamic-update-slice_fusion.19) | copy-start | bytes 288004
  42.2 1.0 %copy-start.21 = (f32[6]{0:T(128)S(1)}, f32[6]{0:T(128)}, u32[]{:S(2)}) copy-start(f32[6]{0:T(128)} %constant.170) | copy-start | bytes 76
  42.2 1.0 %copy-start.31 = (f32[6]{0:T(128)S(1)}, f32[6]{0:T(128)}, u32[]{:S(2)}) copy-start(f32[6]{0:T(128)} %constant.179) | copy-start | bytes 76
  42.2 1.0 %copy-start.32 = (f32[6]{0:T(128)S(1)}, f32[6]{0:T(128)}, u32[]{:S(2)}) copy-start(f32[6]{0:T(128)} %constant.178) | copy-start | bytes 76
  42.4 1.7 %copy-start.18 = (f32[6]{0:T(128)S(1)}, f32[6]{0:T(128)}, u32[]{:S(2)}) copy-start(f32[6]{0:T(128)} %constant.172) | copy-start | bytes 76
  42.4 1.6 %copy-start.28 = (f32[6]{0:T(128)S(1)}, f32[6]{0:T(128)}, u32[]{:S(2)}) copy-start(f32[6]{0:T(128)} %constant.180) | copy-start | bytes 76
  43.2 1.5 %copy-start.19 = (f32[6]{0:T(128)S(1)}, f32[6]{0:T(128)}, u32[]{:S(2)}) copy-start(f32[6]{0:T(128)} %constant.174) | copy-start | bytes 76
  46.4 0.7 copy-start.17
  47.1 0.7 copy-start.24
  47.1 4.7 %copy-start.2 = (f32[125,160]{0,1:T(8,128)S(1)}, f32[125,160]{0,1:T(8,128)}, u32[]{:S(2)}) copy-start(f32[125,160]{0,1:T(8,128)} %get-tuple-element.78) | copy-start | bytes 240004
  47.1 4.7 %copy-start.3 = (f32[125,160]{0,1:T(8,128)S(1)}, f32[125,160]{0,1:T(8,128)}, u32[]{:S(2)}) copy-start(f32[125,160]{0,1:T(8,128)} %get-tuple-element.76) | copy-start | bytes 240004
  47.1 4.7 %copy-start.13 = (f32[125,5,32]{0,2,1:T(8,128)S(1)}, f32[125,5,32]{0,2,1:T(8,128)}, u32[]{:S(2)}) copy-start(f32[125,5,32]{0,2,1:T(8,128)} %constant_dynamic-update-slice_fusion.4) | copy-start | bytes 240004
  48.4 7.3 %all-to-all-start.1 = ((f32[5,125,12]{1,0,2:T(8,128)}), f32[5,125,12]{1,0,2:T(8,128)S(1)}, u32[]{:S(2)}, u32[]{:S(2)}) async-start(f32[5,125,12]{1,0,2:T(8,128)} %fusion.55), calls=%async_computation.1 | async-start | bytes 98304 | tf_op jit(solution)/shard_map/all_to_all | solution.py:324
  51.8 0.9 %copy-start.9 = (f32[150,375]{1,0:T(8,128)S(1)}, f32[150,375]{1,0:T(8,128)}, u32[]{:S(2)}) copy-start(f32[150,375]{1,0:T(8,128)} %constant.164.clone) | copy-start | bytes 675004
  51.9 6.4 %copy-start.10 = (f32[125,375]{1,0:T(8,128)S(1)}, f32[125,375]{1,0:T(8,128)}, u32[]{:S(2)}) copy-start(f32[125,375]{1,0:T(8,128)} %constant.165.clone) | copy-start | bytes 562504
  53.2 10.8 %copy-start.27 = (pred[192]{0:T(512)(128)(4,1)S(1)}, pred[192]{0:T(512)(128)(4,1)}, u32[]{:S(2)}) copy-start(pred[192]{0:T(512)(128)(4,1)} %copy-done.26) | copy-start | bytes 580
  55.8 3.7 %collective-permute-start.4 = (f32[125,12]{0,1:T(8,128)S(1)}, f32[125,12]{0,1:T(8,128)S(1)}, u32[]{:S(2)}, u32[]{:S(2)}) collective-permute-start(f32[125,12]{0,1:T(8,128)S(1)} %bitcast.123), channel_id=1, source_target_pairs={{4,0},{6,2},{8,4},{10,6},{12,8},{14,10},{16,12},{18,14},{20,16},{2... | collective-permute-start | bytes 18008 | tf_op jit(solution)/shard_map/ppermute | solution.py:19
  55.9 3.6 %collective-permute-start.5 = (f32[125,12]{0,1:T(8,128)S(1)}, f32[125,12]{0,1:T(8,128)S(1)}, u32[]{:S(2)}, u32[]{:S(2)}) collective-permute-start(f32[125,12]{0,1:T(8,128)S(1)} %bitcast.124), channel_id=1, source_target_pairs={{2,0},{4,2},{6,4},{8,6},{10,8},{12,10},{14,12},{16,14},{18,16},{20... | collective-permute-start | bytes 18008 | tf_op jit(solution)/shard_map/ppermute | solution.py:19
  55.9 5.8 %collective-permute-start.6 = (f32[125,12]{0,1:T(8,128)S(1)}, f32[125,12]{0,1:T(8,128)S(1)}, u32[]{:S(2)}, u32[]{:S(2)}) collective-permute-start(f32[125,12]{0,1:T(8,128)S(1)} %bitcast.126), channel_id=1, source_target_pairs={{30,0},{0,2},{2,4},{4,6},{6,8},{8,10},{10,12},{12,14},{14,16},{16,... | collective-permute-start | bytes 18008 | tf_op jit(solution)/shard_map/ppermute | solution.py:19
  56.4 6.3 %collective-permute-start.7 = (f32[125,12]{0,1:T(8,128)S(1)}, f32[125,12]{0,1:T(8,128)S(1)}, u32[]{:S(2)}, u32[]{:S(2)}) collective-permute-start(f32[125,12]{0,1:T(8,128)S(1)} %bitcast.128), channel_id=1, source_target_pairs={{28,0},{30,2},{0,4},{2,6},{4,8},{6,10},{8,12},{10,14},{12,16},{14,... | collective-permute-start | bytes 18008 | tf_op jit(solution)/shard_map/ppermute | solution.py:19
  63.0 1.4 %copy-start.20 = (f32[6]{0:T(128)S(1)}, f32[6]{0:T(128)}, u32[]{:S(2)}) copy-start(f32[6]{0:T(128)} %constant.174) | copy-start | bytes 76
  63.0 1.4 %copy-start.22 = (f32[6]{0:T(128)S(1)}, f32[6]{0:T(128)}, u32[]{:S(2)}) copy-start(f32[6]{0:T(128)} %constant.170) | copy-start | bytes 76
  63.0 1.4 %copy-start.30 = (f32[6]{0:T(128)S(1)}, f32[6]{0:T(128)}, u32[]{:S(2)}) copy-start(f32[6]{0:T(128)} %constant.177) | copy-start | bytes 76
  64.4 0.9 %copy-start.7 = (f32[25,1,6,32]{3,0,1,2:T(8,128)S(1)}, f32[25,1,6,32]{3,0,1,2:T(8,128)}, u32[]{:S(2)}) copy-start(f32[25,1,6,32]{3,0,1,2:T(8,128)} %get-tuple-element.29) | copy-start | bytes 57604
  64.5 1.0 %copy-start.5 = (f32[25,1,6,32]{3,0,1,2:T(8,128)S(1)}, f32[25,1,6,32]{3,0,1,2:T(8,128)}, u32[]{:S(2)}) copy-start(f32[25,1,6,32]{3,0,1,2:T(8,128)} %get-tuple-element.25) | copy-start | bytes 57604
  64.8 0.9 %copy-start.6 = (f32[25,1,6,32]{3,0,1,2:T(8,128)S(1)}, f32[25,1,6,32]{3,0,1,2:T(8,128)}, u32[]{:S(2)}) copy-start(f32[25,1,6,32]{3,0,1,2:T(8,128)} %get-tuple-element.23) | copy-start | bytes 57604
  65.4 0.9 %copy-start.4 = (f32[25,1,6,32]{3,0,1,2:T(8,128)S(1)}, f32[25,1,6,32]{3,0,1,2:T(8,128)}, u32[]{:S(2)}) copy-start(f32[25,1,6,32]{3,0,1,2:T(8,128)} %get-tuple-element.21) | copy-start | bytes 57604
  66.5 0.9 %copy-start.12 = (f32[125,150]{1,0:T(8,128)S(1)}, f32[125,150]{1,0:T(8,128)}, u32[]{:S(2)}) copy-start(f32[125,150]{1,0:T(8,128)} %constant.166.clone) | copy-start | bytes 225004
where the time goes:
time: 69.2 us; the launch traced here: 68.6 us
  local copies, waits for them, and re-layouts  19.8 us (29%)
  starting transfers between devices  15.7 us (23%)
  other arithmetic  14.4 us (21%)
  waiting for transfers between devices  13.7 us (20%)
  matrix products  4.2 us (6%)
  between operations  0.76 us (1%)
    ppermute x8, waiting for transfers between devices, passed_along(): return lax.ppermute(block, axis, route)  10.1 us
    ppermute x8, starting transfers between devices, passed_along(): return lax.ppermute(block, axis, route)  8.19 us
    all_to_all x2, starting transfers between devices, shards(): lax.all_to_all(shipment, 'sub', split_axis=2, concat_axis=2, tiled=True)  7.51 us
    sort x2, other arithmetic, group_rank(): ordering = jnp.argsort(group_of * span + sort_key)  6.34 us
    unnamed x78, local copies, waits for them, and re-layouts  4.87 us
    dot_general x6, matrix products, exact_dot(): jnp.dot(matrix, operand, precision=lax.Precision.HIGHEST, preferred_eleme...  3.63 us
    all_to_all x2, waiting for transfers between devices, shards(): lax.all_to_all(shipment, 'sub', split_axis=2, concat_axis=2, tiled=True)  3.58 us
    gather x2, local copies, waits for them, and re-layouts, group_rank(): sorted_group = group_of[ordering]  3.22 us
  transfers between devices with their start and end apart: 10, of which 9 were waited for; matrix products, arithmetic and copies ran while one was open for 7% of the time, Pallas kernels for 0%

commit v1 on v0

v1 whole, which is shorter than its diff:
```python
import jax
import jax.numpy as jnp
import numpy as np
import functools

from jax import lax
from jax.experimental import pallas as pl
from jax.experimental.pallas import tpu as pltpu
from jax.sharding import PartitionSpec as P

ORDER = 4


heat_ratio = 1.4
viscosity = 0.08
prandtl = 0.72
penalty = 0.1


def legendre_table(degree, abscissae):
    values = [abscissae * 0.0 + 1.0, abscissae.copy()]
    slopes = [abscissae * 0.0, abscissae * 0.0 + 1.0]
    for current in range(1, degree):
        values.append(
            ((2 * current + 1) * abscissae * values[current] - current * values[current - 1])
            / (current + 1)
        )
        slopes.append(slopes[current - 1] + (2 * current + 1) * values[current])
    return (values, slopes)


def gauss_nodes(degree):
    abscissae = np.cos(np.pi * (np.arange(degree) + 0.75) / (degree + 0.5))
    for unused in range(60):
        values, slopes = legendre_table(degree, abscissae)
        abscissae = abscissae - values[degree] / slopes[degree]
    return np.sort(abscissae)


def operator_tables(degree):
    abscissae = gauss_nodes(degree)
    differ = abscissae[:, None] - abscissae[None, :]
    padded = differ + np.eye(degree)
    weights = 1.0 / np.prod(padded, axis=1)
    derivative = weights[None, :] / weights[:, None] / padded * (1.0 - np.eye(degree))
    derivative = derivative - np.eye(degree) * np.sum(derivative, axis=1)[:, None]
    basis_left = weights / (-1.0 - abscissae)
    basis_left = basis_left / np.sum(basis_left)
    basis_right = weights / (1.0 - abscissae)
    basis_right = basis_right / np.sum(basis_right)
    values, slopes = legendre_table(degree, abscissae)
    right_slope = 0.5 * (slopes[degree - 1] + slopes[degree])
    mirror_values, mirror_slopes = legendre_table(degree, -abscissae)
    left_slope = -0.5 * (mirror_slopes[degree - 1] + mirror_slopes[degree])
    sol_points = degree**3
    face_points = degree**2
    interp = np.zeros((6 * face_points, sol_points))
    grad_matrix = np.zeros((3 * sol_points, sol_points))
    lift_matrix = np.zeros((3 * sol_points, 6 * face_points))
    div_lift = np.zeros((sol_points, 6 * face_points))
    for sol_index in range(sol_points):
        position = (sol_index // face_points, sol_index // degree % degree, sol_index % degree)
        for direction in range(3):
            others = [position[other_dir] for other_dir in range(3) if other_dir != direction]
            flux_index = others[0] * degree + others[1]
            along_index = position[direction]
            for facing in range(2):
                column = (2 * direction + facing) * face_points + flux_index
                interp[column, sol_index] = (basis_left, basis_right)[facing][along_index]
                correct = (left_slope, right_slope)[facing][along_index]
                lift_matrix[direction * sol_points + sol_index, column] = correct
                div_lift[sol_index, column] = (2 * facing - 1) * correct
            for target in range(degree):
                shifted = list(position)
                shifted[direction] = target
                other_point = (shifted[0] * degree + shifted[1]) * degree + shifted[2]
                grad_matrix[direction * sol_points + sol_index, other_point] = derivative[
                    along_index, target
                ]
    normal_matrix = np.zeros((6 * face_points, 3 * sol_points))
    normals = np.zeros((3, 6))
    for face_id in range(6):
        direction = face_id // 2
        orient = 2 * (face_id % 2) - 1
        rows_here = slice(face_id * face_points, (face_id + 1) * face_points)
        normal_matrix[rows_here, direction * sol_points : (direction + 1) * sol_points] = (
            orient * interp[rows_here]
        )
        normals[direction, face_id] = orient
    div_matrix = np.concatenate(
        [
            grad_matrix[direction * sol_points : (direction + 1) * sol_points]
            for direction in range(3)
        ],
        axis=1,
    )
    tables = (interp, grad_matrix, lift_matrix, normal_matrix, div_matrix, div_lift, normals)
    return tables


FACE_LANES = 32
LANES = 256
ROWS = 8
MESH = pl.DeviceIdType.MESH


def halves(table):
    high = np.asarray(table, dtype=jnp.bfloat16)
    low = np.asarray(table - high.astype(np.float64), dtype=jnp.bfloat16)
    return (high, low)


def kernel_tables():
    interp, grad_matrix, lift_matrix, normal_matrix, div_matrix, div_lift, normals = (
        operator_tables(ORDER + 1)
    )
    side = ORDER + 1
    points, face_points = side**3, side**2
    width = 128
    to_lanes = np.zeros((6 * face_points, LANES))
    for face_id in range(6):
        for point in range(face_points):
            to_lanes[face_id * face_points + point, face_id * FACE_LANES + point] = 1.0
    filled = to_lanes.copy()
    spare = to_lanes.sum(axis=0) == 0.0
    filled[0, spare] = 1.0
    trace = np.zeros((width, LANES))
    trace[:points] = interp.T @ filled
    own_grad = np.zeros((width, 3 * width))
    own_spread = np.zeros((width, 3 * LANES))
    jump_grad = np.zeros((LANES, 3 * width))
    jump_spread = np.zeros((LANES, 3 * LANES))
    div = np.zeros((3 * width, width))
    div_all = div_matrix - div_lift @ normal_matrix
    for direction in range(3):
        rows = slice(direction * points, (direction + 1) * points)
        cols = slice(direction * width, direction * width + points)
        wide = slice(direction * LANES, (direction + 1) * LANES)
        own_grad[:points, cols] = grad_matrix[rows].T
        own_spread[:points, wide] = (interp @ grad_matrix[rows]).T @ to_lanes
        jump_grad[:, cols] = to_lanes.T @ (0.5 * lift_matrix[rows]).T
        jump_spread[:, wide] = to_lanes.T @ (interp @ (0.5 * lift_matrix[rows])).T @ to_lanes
        div[cols, :points] = div_all[:, rows].T
    lift = np.zeros((LANES, width))
    lift[:, :points] = to_lanes.T @ div_lift.T
    result = []
    for table in (trace, own_grad, own_spread, jump_grad, jump_spread, div, lift):
        result.extend(halves(table))
    weights = np.zeros((8, LANES), np.float32)
    for direction in range(3):
        for face_id in range(6):
            start = face_id * FACE_LANES
            weights[direction, start : start + FACE_LANES] = normals[direction, face_id]
    return result + [weights]


def split(value):
    high = value.astype(jnp.bfloat16)
    low = (value - high.astype(jnp.float32)).astype(jnp.bfloat16)
    return (high, low)


def mxu(left, right):
    return jnp.dot(left, right, preferred_element_type=jnp.float32)


def table_dot(parts, high, low):
    return mxu(parts[0], high) + mxu(parts[1], high) + mxu(parts[0], low)


def pick_dot(picks, parts):
    return mxu(picks, parts[0]) + mxu(picks, parts[1])


def faces_first(blocks, lane, elements):
    per_face = []
    for face_id in range(6):
        tile, inner = divmod(face_id * FACE_LANES, 128)
        total = jnp.zeros((elements, 128), jnp.float32)
        for field_id, block in enumerate(blocks):
            if block is None:
                continue
            shift = (25 * field_id - inner) % 128
            piece = block[:, tile * 128 : tile * 128 + 128]
            if shift:
                piece = pltpu.roll(piece, shift, 1)
            mine = (lane >= 25 * field_id) & (lane < 25 * field_id + 25)
            total = jnp.where(mine, piece, total)
        per_face.append(total)
    return jnp.concatenate(per_face, axis=0)


def fields_first(rows, lane, elements, field_ids, base):
    result = []
    for field_id in field_ids:
        tiles = []
        for tile in range(2):
            total = base[field_id][:, tile * 128 : tile * 128 + 128]
            for face_id in range(tile * 4, min(6, tile * 4 + 4)):
                inner = face_id * FACE_LANES - tile * 128
                shift = (inner - 25 * field_id) % 128
                piece = rows[face_id * elements : (face_id + 1) * elements]
                if shift:
                    piece = pltpu.roll(piece, shift, 1)
                mine = (lane >= inner) & (lane < inner + 25)
                total = jnp.where(mine, piece, total)
            tiles.append(total)
        result.append(jnp.concatenate(tiles, axis=1))
    return result


def divided(value, count):
    return jnp.floor((value + 0.5) * (1.0 / count))


def state_of(fields):
    inverse = 1.0 / fields[0]
    velocity = [fields[1 + b] * inverse for b in range(3)]
    kinetic = 0.5 * (fields[1] * velocity[0] + fields[2] * velocity[1] + fields[3] * velocity[2])
    pressure = (heat_ratio - 1.0) * (fields[4] - kinetic)
    return (inverse, velocity, pressure)


def normal_inviscid(fields, velocity, pressure, normal):
    speed = sum(normal[b] * velocity[b] for b in range(3))
    momentum = sum(normal[b] * fields[1 + b] for b in range(3))
    flux = [momentum]
    for b in range(3):
        flux.append(fields[1 + b] * speed + pressure * normal[b])
    flux.append((fields[4] + pressure) * speed)
    return (flux, speed)


def slopes_of(fields, inverse, velocity, grads):
    slope = [
        [(grads[a][1 + b] - velocity[b] * grads[a][0]) * inverse for a in range(3)]
        for b in range(3)
    ]
    specific = fields[4] * inverse
    energy = []
    for a in range(3):
        value = (grads[a][4] - specific * grads[a][0]) * inverse
        energy.append(value - sum(velocity[b] * slope[b][a] for b in range(3)))
    return (slope, energy)


def body(shape, *refs):
    elements, capacity, sub_count, dom_count = shape
    sol_ref, link_ref = refs[:2]
    (trace_h, trace_l, own_grad_h, own_grad_l, own_spread_h, own_spread_l, jump_grad_h,
     jump_grad_l, jump_spread_h, jump_spread_l, div_h, div_l, lift_h, lift_l) = refs[2:16]
    weights_ref, out_ref, padded, outbox, inbox, send_sem, recv_sem = refs[16:]
    my_dom, my_sub = lax.axis_index("dom"), lax.axis_index("sub")
    home = 2 * sub_count
    groups = 5 * sub_count
    partners = []
    for offset in range(-2, 3):
        for across in range(sub_count):
            if offset == 0 and across == 0:
                continue
            there = (
                lax.rem(my_dom + offset + dom_count, dom_count),
                lax.rem(my_sub + across, sub_count),
            )
            group = (offset + 2) * sub_count + across
            mirror = (2 - offset) * sub_count + (-across) % sub_count
            partners.append((group, mirror, there))
    barrier = pltpu.get_barrier_semaphore()
    for _, _, there in partners:
        pl.semaphore_signal(barrier, inc=1, device_id=there, device_id_type=MESH)

    def ship(turn):
        copies = []
        for group, mirror, there in partners:
            copies.append(
                pltpu.make_async_remote_copy(
                    src_ref=outbox.at[turn, group],
                    dst_ref=inbox.at[turn, mirror],
                    send_sem=send_sem.at[turn, group],
                    recv_sem=recv_sem.at[turn, mirror],
                    device_id=there,
                    device_id_type=MESH,
                )
            )
            copies[-1].start()
        return copies

    faces = 6 * elements
    slots = groups * ROWS
    points = sol_ref.shape[2]
    lane = lax.broadcasted_iota(jnp.int32, (elements, 128), 1)

    for k in range(5):
        here = sol_ref[k]
        padded[k * elements : (k + 1) * elements, :points] = here
        padded[k * elements : (k + 1) * elements, points:] = here[:, : 128 - points]
    state = padded[...]
    state_parts = split(state)
    own = table_dot(state_parts, trace_h[...], trace_l[...])

    def by_field(values, start=0, width=LANES):
        return [
            values[k * elements : (k + 1) * elements, start : start + width] for k in range(5)
        ]

    own_fields = by_field(own)
    own_rows = faces_first(own_fields, lane, elements)
    own_parts = split(own_rows)

    link = link_ref[...].astype(jnp.float32)
    elem = divided(link, 6)
    side = link - 6.0 * elem
    device = divided(elem, elements)
    key = side * elements + (elem - device * elements)
    dom = divided(device, sub_count)
    sub = device - dom * sub_count
    ahead = dom - my_dom.astype(jnp.float32) + 2.0
    ahead = jnp.where(ahead < 0.0, ahead + dom_count, ahead)
    ahead = jnp.where(ahead >= dom_count, ahead - dom_count, ahead)
    across = sub - my_sub.astype(jnp.float32)
    across = jnp.where(across < 0.0, across + sub_count, across)
    group = ahead * sub_count + across

    def as_row(value):
        return jnp.concatenate([value[f : f + 1] for f in range(6)], axis=1)

    group_row = as_row(group)
    key_row = as_row(key)
    both = jnp.concatenate([group_row, key_row] + [group_row] * 6, axis=0).T
    group_col = both[:, 0:1]
    key_col = both[:, 1:2]
    down = lax.broadcasted_iota(jnp.int32, (faces, faces), 0)
    along = lax.broadcasted_iota(jnp.int32, (faces, faces), 1)
    same = group_col == group_row
    send_rank = jnp.sum(jnp.where(same & (down < along), 1.0, 0.0), axis=0, keepdims=True)
    send_slot = jnp.where(group_row == home, -1.0, group_row * ROWS + send_rank)
    slot_down = lax.broadcasted_iota(jnp.int32, (slots, faces), 0).astype(jnp.float32)
    send_pick = jnp.where(send_slot == slot_down, 1.0, 0.0).astype(jnp.bfloat16)

    outbox[0] = pick_dot(send_pick, own_parts).reshape(groups, ROWS, 128)
    pl.semaphore_wait(barrier, len(partners))
    first = ship(0)

    recv_rank = jnp.sum(jnp.where(same & (key_row < key_col), 1.0, 0.0), axis=1, keepdims=True)
    recv_slot = jnp.where(group_col == home, -1.0, group_col * ROWS + recv_rank)
    slot_along = lax.broadcasted_iota(jnp.int32, (faces, slots), 1).astype(jnp.float32)
    recv_pick = jnp.where(recv_slot == slot_along, 1.0, 0.0).astype(jnp.bfloat16)
    near_key = jnp.where(group_col == home, key_col, -1.0)
    near_pick = jnp.where(near_key == along.astype(jnp.float32), 1.0, 0.0).astype(jnp.bfloat16)

    near_rows = pick_dot(near_pick, own_parts)
    own_spread = table_dot(state_parts, own_spread_h[...], own_spread_l[...])
    own_grad = table_dot(state_parts, own_grad_h[...], own_grad_l[...])
    normal = [weights_ref[a : a + 1] for a in range(3)]
    inverse, velocity, pressure = state_of(own_fields)
    own_flux, own_speed = normal_inviscid(own_fields, velocity, pressure, normal)
    own_wave = jnp.abs(own_speed) + jnp.sqrt(heat_ratio * pressure * inverse)

    inbox[0, home] = jnp.zeros((ROWS, 128), jnp.float32)
    inbox[1, home] = jnp.zeros((ROWS, 128), jnp.float32)
    for copy in first:
        copy.wait_recv()
    arrived = split(inbox[0].reshape(slots, 128))
    other_rows = near_rows + pick_dot(recv_pick, arrived)
    other_fields = fields_first(other_rows, lane, elements, range(5), own_fields)
    jump = jnp.concatenate([other_fields[k] - own_fields[k] for k in range(5)], axis=0)
    jump_parts = split(jump)
    spread = own_spread + table_dot(jump_parts, jump_spread_h[...], jump_spread_l[...])
    grads = [by_field(spread, a * LANES) for a in range(3)]

    slope, energy = slopes_of(own_fields, inverse, velocity, grads)
    divergence = slope[0][0] + slope[1][1] + slope[2][2]
    own_visc = [None]
    for b in range(3):
        stress = sum(normal[a] * (slope[b][a] + slope[a][b]) for a in range(3))
        own_visc.append(viscosity * stress - (2.0 / 3.0 * viscosity) * normal[b] * divergence)
    heat = sum(normal[a] * energy[a] for a in range(3))
    own_visc.append(
        sum(velocity[b] * own_visc[1 + b] for b in range(3))
        + (viscosity * heat_ratio / prandtl) * heat
    )
    visc_rows = faces_first(own_visc, lane, elements)
    visc_parts = split(visc_rows)
    outbox[1] = pick_dot(send_pick, visc_parts).reshape(groups, ROWS, 128)
    second = ship(1)

    near_visc = pick_dot(near_pick, visc_parts)
    grad = own_grad + table_dot(jump_parts, jump_grad_h[...], jump_grad_l[...])
    grads = [by_field(grad, a * 128, 128) for a in range(3)]
    fields = by_field(state, 0, 128)
    inner_inverse, inner_velocity, inner_pressure = state_of(fields)
    slope, energy = slopes_of(fields, inner_inverse, inner_velocity, grads)
    divergence = (2.0 / 3.0 * viscosity) * (slope[0][0] + slope[1][1] + slope[2][2])
    total = None
    for a in range(3):
        stress = []
        for b in range(3):
            if a == b:
                stress.append((2.0 * viscosity) * slope[a][a] - divergence)
            else:
                stress.append(viscosity * (slope[b][a] + slope[a][b]))
        flux = [fields[1 + a]]
        for b in range(3):
            member = fields[1 + b] * inner_velocity[a] - stress[b]
            flux.append(member + inner_pressure if a == b else member)
        flux.append(
            (fields[4] + inner_pressure) * inner_velocity[a]
            - sum(inner_velocity[b] * stress[b] for b in range(3))
            - (viscosity * heat_ratio / prandtl) * energy[a]
        )
        flux_parts = split(jnp.concatenate(flux, axis=0))
        rows = slice(a * 128, (a + 1) * 128)
        part = table_dot(flux_parts, div_h[rows], div_l[rows])
        total = part if total is None else total + part

    other_inverse, other_velocity, other_pressure = state_of(other_fields)
    other_flux, other_speed = normal_inviscid(
        other_fields, other_velocity, other_pressure, normal
    )
    other_wave = jnp.abs(other_speed) + jnp.sqrt(heat_ratio * other_pressure * other_inverse)
    factor = 0.5 * jnp.maximum(own_wave, other_wave) + penalty
    common = []
    for k in range(5):
        member = 0.5 * (own_flux[k] + other_flux[k]) + factor * (own_fields[k] - other_fields[k])
        common.append(member if k == 0 else member - 0.5 * own_visc[k])
    total = total + table_dot(split(jnp.concatenate(common, axis=0)), lift_h[...], lift_l[...])

    for copy in second:
        copy.wait_recv()
    arrived = split(0.5 * inbox[1].reshape(slots, 128))
    other_rows = 0.5 * near_visc + pick_dot(recv_pick, arrived)
    zeros = [jnp.zeros((elements, LANES), jnp.float32)] * 5
    other_visc = fields_first(other_rows, lane, elements, range(1, 5), zeros)
    lifted = table_dot(split(jnp.concatenate(other_visc, axis=0)), lift_h[...], lift_l[...])
    out_ref[0] = -total[:elements, :points]
    for k in range(1, 5):
        rows = slice(k * elements, (k + 1) * elements)
        near = slice((k - 1) * elements, k * elements)
        out_ref[k] = -(total[rows, :points] + lifted[near, :points])
    for copy in first + second:
        copy.wait_send()


def shards(solution, face_link):
    points, fields, elements = solution.shape
    sub_count = lax.axis_size("sub")
    dom_count = lax.axis_size("dom")
    capacity = max(3, elements * 3 // 16)
    assert capacity <= ROWS
    groups = 5 * sub_count
    tables = [jnp.asarray(table) for table in kernel_tables()]
    vmem = pl.BlockSpec(memory_space=pltpu.VMEM)
    rate = pl.pallas_call(
        functools.partial(body, (elements, capacity, sub_count, dom_count)),
        out_shape=jax.ShapeDtypeStruct((fields, elements, points), jnp.float32),
        in_specs=[vmem] * (2 + len(tables)),
        out_specs=vmem,
        scratch_shapes=[
            pltpu.VMEM((fields * elements, 128), jnp.float32),
            pltpu.VMEM((2, groups, ROWS, 128), jnp.float32),
            pltpu.VMEM((2, groups, ROWS, 128), jnp.float32),
            pltpu.SemaphoreType.DMA((2, groups)),
            pltpu.SemaphoreType.DMA((2, groups)),
        ],
        compiler_params=pltpu.CompilerParams(collective_id=0, has_side_effects=True),
    )(jnp.transpose(solution, (1, 2, 0)), face_link, *tables)
    return jnp.transpose(rate, (2, 0, 1))


def solution(mesh):
    in_specs = (P(None, None, ("dom", "sub")), P(None, ("dom", "sub")))
    out_specs = P(None, None, ("dom", "sub"))
    return jax.shard_map(shards, mesh=mesh, in_specs=in_specs, out_specs=out_specs, check_vma=False)
```

time: 69.2 us -> 21.9 us (0.32)
  Pallas kernels: 0 us -> 20.2 us
  local copies, waits for them, and re-layouts: 19.8 us -> 1.53 us
  starting transfers between devices: 15.7 us -> 0 us
  other arithmetic: 14.4 us -> 0 us
  waiting for transfers between devices: 13.7 us -> 0 us
  matrix products: 4.2 us -> 0 us
  between operations: 0.76 us -> 0.01 us
    pallas_call x0 -> x1, Pallas kernels: none -> 20.2 us  [shards(): pl.pallas_call(functools.partial(body, (elements, capacity, sub_count, do...]
    ppermute x8 -> x0, waiting for transfers between devices: 10.1 us -> none  [passed_along(): return lax.ppermute(block, axis, route)]
    ppermute x8 -> x0, starting transfers between devices: 8.19 us -> none  [passed_along(): return lax.ppermute(block, axis, route)]
    all_to_all x2 -> x0, starting transfers between devices: 7.51 us -> none  [shards(): lax.all_to_all(shipment, 'sub', split_axis=2, concat_axis=2, tiled=True)]
    sort x2 -> x0, other arithmetic: 6.34 us -> none  [group_rank(): ordering = jnp.argsort(group_of * span + sort_key)]
    gather x8 -> x0, local copies, waits for them, and re-layouts: 6.07 us -> none  [the longest x2 3.22 us: group_rank(): sorted_group = group_of[ordering]]
    dot_general x7 -> x0, matrix products: 4.2 us -> none  [the longest x6 3.63 us: exact_dot(): jnp.dot(matrix, operand, precision=lax.Precision.HIGHEST, preferred_eleme...]
    scatter x3 -> x0, local copies, waits for them, and re-layouts: 3.58 us -> none  [the longest x2 2.39 us: group_rank(): return jnp.zeros((length,), jnp.int32).at[ordering].set(ranked)]
  transfers between devices with their start and end apart: 10 -> 0, of which waited for: 9 -> 0; matrix products, arithmetic and copies ran while one was open for 7% -> 0% of each run, Pallas kernels for 0% -> 0%
where the time goes in v1:
time: 21.9 us; the launch traced here: 21.7 us
  Pallas kernels  20.2 us (92%)
  local copies, waits for them, and re-layouts  1.53 us (7%)
    pallas_call x1, Pallas kernels, shards(): pl.pallas_call(functools.partial(body, (elements, capacity, sub_count, do...  20.2 us
    unnamed x1, local copies, waits for them, and re-layouts  1.53 us

profile of v1, /device:TPU:0, one launch (start us, length us, event | category | flops | bytes accessed | tf_op | source)
XLA Modules:
  0.0 21.7 jit_solution(5560575237451291945)
XLA Ops:
  0.0 20.2 %shard_map.163 = f32[5,32,125]{2,1,0:T(8,128)} custom-call(f32[5,32,125]{2,1,0:T(8,128)} %bitcast.3, s32[6,32]{1,0:T(8,128)} %refs_1_.1, bf16[128,256]{1,0:T(8,128)(2,1)} %constant.30.clone.refs_2_, bf16[128,256]{1,0:T(8,128)(2,1)} %constant.31.clone.refs_3_, bf16[128,384]{1,0:T(8,128)(2,1)} %constant.32.clone.refs_4_, ...), custom_call_target="tpu_custom_call" | custom-call | tf_op jit(solution)/shard_map/pallas_call | solution.py:453
  20.2 1.5 %copy.19 = f32[125,5,32]{0,2,1:T(8,128)} copy(f32[125,5,32]{0,2,1:T(8,128)} %bitcast.2) | data formatting | bytes 160000

commit v2 on v1

--- a/solution.py
+++ b/solution.py
@@ -145,7 +145,7 @@
     lift[:, :points] = to_lanes.T @ div_lift.T
     result = []
     for table in (trace, own_grad, own_spread, jump_grad, jump_spread, div, lift):
-        result.extend(halves(table))
+        result.append(np.stack(halves(table)))
     weights = np.zeros((8, LANES), np.float32)
     for direction in range(3):
         for face_id in range(6):
@@ -160,6 +160,12 @@
     return (high, low)
 
 
+def thirds(value):
+    high, low = split(value)
+    rest = value - high.astype(jnp.float32) - low.astype(jnp.float32)
+    return (high, low, rest.astype(jnp.bfloat16))
+
+
 def mxu(left, right):
     return jnp.dot(left, right, preferred_element_type=jnp.float32)
 
@@ -169,7 +175,7 @@
 
 
 def pick_dot(picks, parts):
-    return mxu(picks, parts[0]) + mxu(picks, parts[1])
+    return sum(mxu(picks, part) for part in parts)
 
 
 def faces_first(blocks, lane, elements):
@@ -246,10 +252,10 @@
 
 def body(shape, *refs):
     elements, capacity, sub_count, dom_count = shape
-    sol_ref, link_ref = refs[:2]
-    (trace_h, trace_l, own_grad_h, own_grad_l, own_spread_h, own_spread_l, jump_grad_h,
-     jump_grad_l, jump_spread_h, jump_spread_l, div_h, div_l, lift_h, lift_l) = refs[2:16]
-    weights_ref, out_ref, padded, outbox, inbox, send_sem, recv_sem = refs[16:]
+    far, out_ref, held = refs[:10], refs[10], refs[11:21]
+    padded, outbox, inbox, load_sem, send_sem, recv_sem = refs[21:]
+    sol_ref, link_ref, trace, own_grad_t, own_spread_t, jump_grad, jump_spread, div, lift = held[:9]
+    weights_ref = held[9]
     my_dom, my_sub = lax.axis_index("dom"), lax.axis_index("sub")
     home = 2 * sub_count
     groups = 5 * sub_count
@@ -285,18 +291,30 @@
             copies[-1].start()
         return copies
 
+    loads = [
+        pltpu.make_async_copy(far[i], held[i], load_sem.at[i])
+        for i in range(10)
+    ]
+    for i in (0, 1, 2, 4, 3, 9, 6, 5, 7, 8):
+        loads[i].start()
+
+    def loaded(*which):
+        for i in which:
+            loads[i].wait()
+
     faces = 6 * elements
     slots = groups * ROWS
     points = sol_ref.shape[2]
     lane = lax.broadcasted_iota(jnp.int32, (elements, 128), 1)
 
+    loaded(0, 2)
     for k in range(5):
         here = sol_ref[k]
         padded[k * elements : (k + 1) * elements, :points] = here
         padded[k * elements : (k + 1) * elements, points:] = here[:, : 128 - points]
     state = padded[...]
     state_parts = split(state)
-    own = table_dot(state_parts, trace_h[...], trace_l[...])
+    own = table_dot(state_parts, trace[0], trace[1])
 
     def by_field(values, start=0, width=LANES):
         return [
@@ -305,8 +323,9 @@
 
     own_fields = by_field(own)
     own_rows = faces_first(own_fields, lane, elements)
-    own_parts = split(own_rows)
-
+    own_parts = thirds(own_rows)
+
+    loaded(1)
     link = link_ref[...].astype(jnp.float32)
     elem = divided(link, 6)
     side = link - 6.0 * elem
@@ -349,23 +368,25 @@
     near_pick = jnp.where(near_key == along.astype(jnp.float32), 1.0, 0.0).astype(jnp.bfloat16)
 
     near_rows = pick_dot(near_pick, own_parts)
-    own_spread = table_dot(state_parts, own_spread_h[...], own_spread_l[...])
-    own_grad = table_dot(state_parts, own_grad_h[...], own_grad_l[...])
+    loaded(4, 3, 9)
+    own_spread = table_dot(state_parts, own_spread_t[0], own_spread_t[1])
+    own_grad = table_dot(state_parts, own_grad_t[0], own_grad_t[1])
     normal = [weights_ref[a : a + 1] for a in range(3)]
     inverse, velocity, pressure = state_of(own_fields)
     own_flux, own_speed = normal_inviscid(own_fields, velocity, pressure, normal)
     own_wave = jnp.abs(own_speed) + jnp.sqrt(heat_ratio * pressure * inverse)
 
+    loaded(6)
     inbox[0, home] = jnp.zeros((ROWS, 128), jnp.float32)
     inbox[1, home] = jnp.zeros((ROWS, 128), jnp.float32)
     for copy in first:
         copy.wait_recv()
-    arrived = split(inbox[0].reshape(slots, 128))
+    arrived = thirds(inbox[0].reshape(slots, 128))
     other_rows = near_rows + pick_dot(recv_pick, arrived)
     other_fields = fields_first(other_rows, lane, elements, range(5), own_fields)
     jump = jnp.concatenate([other_fields[k] - own_fields[k] for k in range(5)], axis=0)
     jump_parts = split(jump)
-    spread = own_spread + table_dot(jump_parts, jump_spread_h[...], jump_spread_l[...])
+    spread = own_spread + table_dot(jump_parts, jump_spread[0], jump_spread[1])
     grads = [by_field(spread, a * LANES) for a in range(3)]
 
     slope, energy = slopes_of(own_fields, inverse, velocity, grads)
@@ -384,8 +405,9 @@
     outbox[1] = pick_dot(send_pick, visc_parts).reshape(groups, ROWS, 128)
     second = ship(1)
 
+    loaded(5, 7, 8)
     near_visc = pick_dot(near_pick, visc_parts)
-    grad = own_grad + table_dot(jump_parts, jump_grad_h[...], jump_grad_l[...])
+    grad = own_grad + table_dot(jump_parts, jump_grad[0], jump_grad[1])
     grads = [by_field(grad, a * 128, 128) for a in range(3)]
     fields = by_field(state, 0, 128)
     inner_inverse, inner_velocity, inner_pressure = state_of(fields)
@@ -410,7 +432,7 @@
         )
         flux_parts = split(jnp.concatenate(flux, axis=0))
         rows = slice(a * 128, (a + 1) * 128)
-        part = table_dot(flux_parts, div_h[rows], div_l[rows])
+        part = table_dot(flux_parts, div[0, rows], div[1, rows])
         total = part if total is None else total + part
 
     other_inverse, other_velocity, other_pressure = state_of(other_fields)
@@ -423,7 +445,7 @@
     for k in range(5):
         member = 0.5 * (own_flux[k] + other_flux[k]) + factor * (own_fields[k] - other_fields[k])
         common.append(member if k == 0 else member - 0.5 * own_visc[k])
-    total = total + table_dot(split(jnp.concatenate(common, axis=0)), lift_h[...], lift_l[...])
+    total = total + table_dot(split(jnp.concatenate(common, axis=0)), lift[0], lift[1])
 
     for copy in second:
         copy.wait_recv()
@@ -431,12 +453,12 @@
     other_rows = 0.5 * near_visc + pick_dot(recv_pick, arrived)
     zeros = [jnp.zeros((elements, LANES), jnp.float32)] * 5
     other_visc = fields_first(other_rows, lane, elements, range(1, 5), zeros)
-    lifted = table_dot(split(jnp.concatenate(other_visc, axis=0)), lift_h[...], lift_l[...])
-    out_ref[0] = -total[:elements, :points]
+    lifted = table_dot(split(jnp.concatenate(other_visc, axis=0)), lift[0], lift[1])
+    out_ref[0] = total[:elements, :points]
     for k in range(1, 5):
         rows = slice(k * elements, (k + 1) * elements)
         near = slice((k - 1) * elements, k * elements)
-        out_ref[k] = -(total[rows, :points] + lifted[near, :points])
+        out_ref[k] = total[rows, :points] + lifted[near, :points]
     for copy in first + second:
         copy.wait_send()
 
@@ -450,21 +472,24 @@
     groups = 5 * sub_count
     tables = [jnp.asarray(table) for table in kernel_tables()]
     vmem = pl.BlockSpec(memory_space=pltpu.VMEM)
+    operands = [jnp.transpose(solution, (1, 2, 0)), face_link] + tables
+    held = [pltpu.VMEM(operand.shape, operand.dtype) for operand in operands]
     rate = pl.pallas_call(
         functools.partial(body, (elements, capacity, sub_count, dom_count)),
-        out_shape=jax.ShapeDtypeStruct((fields, elements, points), jnp.float32),
-        in_specs=[vmem] * (2 + len(tables)),
+        out_shape=pltpu.VMEM((fields, elements, points), jnp.float32),
+        in_specs=[pl.BlockSpec(memory_space=pltpu.HBM)] * len(operands),
         out_specs=vmem,
-        scratch_shapes=[
+        scratch_shapes=held + [
             pltpu.VMEM((fields * elements, 128), jnp.float32),
             pltpu.VMEM((2, groups, ROWS, 128), jnp.float32),
             pltpu.VMEM((2, groups, ROWS, 128), jnp.float32),
+            pltpu.SemaphoreType.DMA((len(operands),)),
             pltpu.SemaphoreType.DMA((2, groups)),
             pltpu.SemaphoreType.DMA((2, groups)),
         ],
         compiler_params=pltpu.CompilerParams(collective_id=0, has_side_effects=True),
-    )(jnp.transpose(solution, (1, 2, 0)), face_link, *tables)
-    return jnp.transpose(rate, (2, 0, 1))
+    )(*operands)
+    return jnp.transpose(-rate, (2, 0, 1))
 
 
 def solution(mesh):

time: 21.9 us -> 19.1 us (0.87)
  Pallas kernels: 20.2 us -> 18.3 us
  local copies, waits for them, and re-layouts: 1.53 us -> 0 us
  other arithmetic: 0 us -> 0.64 us
    pallas_call x1, Pallas kernels: 20.2 us -> 18.3 us  [shards(): pl.pallas_call(functools.partial(body, (elements, capacity, sub_count, do...]
    unnamed x1 -> x0, local copies, waits for them, and re-layouts: 1.53 us -> none
    transpose x0 -> x1, other arithmetic: none -> 0.64 us  [shards(): return jnp.transpose(-rate, (2, 0, 1))]
where the time goes in v2:
time: 19.1 us; the launch traced here: 19 us
  Pallas kernels  18.3 us (96%)
  other arithmetic  0.64 us (3%)
    pallas_call x1, Pallas kernels, shards(): pl.pallas_call(functools.partial(body, (elements, capacity, sub_count, do...  18.3 us
    transpose x1, other arithmetic, shards(): return jnp.transpose(-rate, (2, 0, 1))  0.64 us

profile of v2, /device:TPU:0, one launch (start us, length us, event | category | flops | bytes accessed | tf_op | source)
XLA Modules:
  0.0 19.0 jit_solution(8064806542372444217)
XLA Ops:
  0.0 18.3 %shard_map.100 = f32[5,32,125]{2,1,0:T(8,128)S(1)} custom-call(f32[5,32,125]{2,1,0:T(8,128)} %bitcast.3, s32[6,32]{1,0:T(8,128)} %refs_1_.1, bf16[2,128,256]{2,1,0:T(8,128)(2,1)} %constant.16.clone.refs_2_, bf16[2,128,384]{2,1,0:T(8,128)(2,1)} %constant.17.clone.refs_3_, bf16[2,128,768]{2,1,0:T(8,128)(2,1)} %constant.18.clone.refs_4_, ...), custom_call_target="tpu_custom_call" | custom-call | tf_op jit(solution)/shard_map/pallas_call | solution.py:477
  18.3 0.6 %negate_bitcast_fusion = f32[125,5,32]{0,2,1:T(8,128)} fusion(f32[5,32,125]{2,1,0:T(8,128)S(1)} %shard_map.100), kind=kLoop, calls=%fused_computation | loop fusion | flops 20000 | bytes 160000 | tf_op jit(solution)/shard_map/transpose | solution.py:492

commit v3 on v2

--- a/solution.py
+++ b/solution.py
@@ -144,8 +144,13 @@
     lift = np.zeros((LANES, width))
     lift[:, :points] = to_lanes.T @ div_lift.T
     result = []
-    for table in (trace, own_grad, own_spread, jump_grad, jump_spread, div, lift):
+    for table in (trace, own_grad, own_spread):
+        result.append(table.astype(np.float32))
+    for table in (jump_grad, jump_spread):
         result.append(np.stack(halves(table)))
+    for table in (div, lift):
+        result.append(table.astype(np.float32))
+    result.append(np.stack(halves(lift)))
     weights = np.zeros((8, LANES), np.float32)
     for direction in range(3):
         for face_id in range(6):
@@ -172,6 +177,12 @@
 
 def table_dot(parts, high, low):
     return mxu(parts[0], high) + mxu(parts[1], high) + mxu(parts[0], low)
+
+
+def full_dot(left, right):
+    return jnp.dot(
+        left, right, precision=lax.Precision.HIGHEST, preferred_element_type=jnp.float32
+    )
 
 
 def pick_dot(picks, parts):
@@ -252,10 +263,10 @@
 
 def body(shape, *refs):
     elements, capacity, sub_count, dom_count = shape
-    far, out_ref, held = refs[:10], refs[10], refs[11:21]
-    padded, outbox, inbox, load_sem, send_sem, recv_sem = refs[21:]
+    far, out_ref, held = refs[:11], refs[11], refs[12:23]
+    padded, outbox, inbox, load_sem, send_sem, recv_sem = refs[23:]
     sol_ref, link_ref, trace, own_grad_t, own_spread_t, jump_grad, jump_spread, div, lift = held[:9]
-    weights_ref = held[9]
+    lift_pair, weights_ref = held[9:]
     my_dom, my_sub = lax.axis_index("dom"), lax.axis_index("sub")
     home = 2 * sub_count
     groups = 5 * sub_count
@@ -293,9 +304,9 @@
 
     loads = [
         pltpu.make_async_copy(far[i], held[i], load_sem.at[i])
-        for i in range(10)
+        for i in range(11)
     ]
-    for i in (0, 1, 2, 4, 3, 9, 6, 5, 7, 8):
+    for i in (0, 1, 2, 4, 3, 10, 6, 5, 7, 8, 9):
         loads[i].start()
 
     def loaded(*which):
@@ -313,8 +324,7 @@
         padded[k * elements : (k + 1) * elements, :points] = here
         padded[k * elements : (k + 1) * elements, points:] = here[:, : 128 - points]
     state = padded[...]
-    state_parts = split(state)
-    own = table_dot(state_parts, trace[0], trace[1])
+    own = full_dot(state, trace[...])
 
     def by_field(values, start=0, width=LANES):
         return [
@@ -368,9 +378,9 @@
     near_pick = jnp.where(near_key == along.astype(jnp.float32), 1.0, 0.0).astype(jnp.bfloat16)
 
     near_rows = pick_dot(near_pick, own_parts)
-    loaded(4, 3, 9)
-    own_spread = table_dot(state_parts, own_spread_t[0], own_spread_t[1])
-    own_grad = table_dot(state_parts, own_grad_t[0], own_grad_t[1])
+    loaded(4, 3, 10)
+    own_spread = full_dot(state, own_spread_t[...])
+    own_grad = full_dot(state, own_grad_t[...])
     normal = [weights_ref[a : a + 1] for a in range(3)]
     inverse, velocity, pressure = state_of(own_fields)
     own_flux, own_speed = normal_inviscid(own_fields, velocity, pressure, normal)
@@ -405,7 +415,7 @@
     outbox[1] = pick_dot(send_pick, visc_parts).reshape(groups, ROWS, 128)
     second = ship(1)
 
-    loaded(5, 7, 8)
+    loaded(5, 7, 8, 9)
     near_visc = pick_dot(near_pick, visc_parts)
     grad = own_grad + table_dot(jump_parts, jump_grad[0], jump_grad[1])
     grads = [by_field(grad, a * 128, 128) for a in range(3)]
@@ -430,9 +440,8 @@
             - sum(inner_velocity[b] * stress[b] for b in range(3))
             - (viscosity * heat_ratio / prandtl) * energy[a]
         )
-        flux_parts = split(jnp.concatenate(flux, axis=0))
         rows = slice(a * 128, (a + 1) * 128)
-        part = table_dot(flux_parts, div[0, rows], div[1, rows])
+        part = full_dot(jnp.concatenate(flux, axis=0), div[rows])
         total = part if total is None else total + part
 
     other_inverse, other_velocity, other_pressure = state_of(other_fields)
@@ -445,7 +454,7 @@
     for k in range(5):
         member = 0.5 * (own_flux[k] + other_flux[k]) + factor * (own_fields[k] - other_fields[k])
         common.append(member if k == 0 else member - 0.5 * own_visc[k])
-    total = total + table_dot(split(jnp.concatenate(common, axis=0)), lift[0], lift[1])
+    total = total + full_dot(jnp.concatenate(common, axis=0), lift[...])
 
     for copy in second:
         copy.wait_recv()
@@ -453,7 +462,7 @@
     other_rows = 0.5 * near_visc + pick_dot(recv_pick, arrived)
     zeros = [jnp.zeros((elements, LANES), jnp.float32)] * 5
     other_visc = fields_first(other_rows, lane, elements, range(1, 5), zeros)
-    lifted = table_dot(split(jnp.concatenate(other_visc, axis=0)), lift[0], lift[1])
+    lifted = table_dot(split(jnp.concatenate(other_visc, axis=0)), lift_pair[0], lift_pair[1])
     out_ref[0] = total[:elements, :points]
     for k in range(1, 5):
         rows = slice(k * elements, (k + 1) * elements)

time: 19.1 us -> 19.4 us (1.016)
  Pallas kernels: 18.3 us -> 18.6 us
    pallas_call x1, Pallas kernels: 18.3 us -> 18.6 us  [shards(): pl.pallas_call(functools.partial(body, (elements, capacity, sub_count, do...]
where the time goes in v3:
time: 19.4 us; the launch traced here: 19.3 us
  Pallas kernels  18.6 us (96%)
  other arithmetic  0.64 us (3%)
    pallas_call x1, Pallas kernels, shards(): pl.pallas_call(functools.partial(body, (elements, capacity, sub_count, do...  18.6 us
    transpose x1, other arithmetic, shards(): return jnp.transpose(-rate, (2, 0, 1))  0.64 us

profile of v3, /device:TPU:0, one launch (start us, length us, event | category | flops | bytes accessed | tf_op | source)
XLA Modules:
  0.0 19.3 jit_solution(17788582916954034195)
XLA Ops:
  0.0 18.6 %shard_map.109 = f32[5,32,125]{2,1,0:T(8,128)S(1)} custom-call(f32[5,32,125]{2,1,0:T(8,128)} %bitcast.3, s32[6,32]{1,0:T(8,128)} %refs_1_.1, f32[128,256]{1,0:T(8,128)} %constant.18.clone.refs_2_, f32[128,384]{1,0:T(8,128)} %constant.19.clone.refs_3_, f32[128,768]{1,0:T(8,128)} %constant.20.clone.refs_4_, bf16[2,256,384]{2,1,0:T(8,128)(2,1)} %constant.21.clone.refs_5_, ...), custom_call_target="tpu_custom_call" | custom-call | tf_op jit(solution)/shard_map/pallas_call | solution.py:486
  18.6 0.6 %negate_bitcast_fusion = f32[125,5,32]{0,2,1:T(8,128)} fusion(f32[5,32,125]{2,1,0:T(8,128)S(1)} %shard_map.109), kind=kLoop, calls=%fused_computation | loop fusion | flops 20000 | bytes 160000 | tf_op jit(solution)/shard_map/transpose | solution.py:501
